TPU v7x, 32 devices: a whole 2x2x4 slice. The times are simulated.
32 devices in a mesh: dp: 8 (over y, x, core), mp: 4 (over z).
Axes of the slice: x: 2, y: 2, z: 4, core: 2. Of those that a mesh axis runs over, the one named last changes fastest.
Arguments:
- grad_parts: bfloat16 [8, 1, 6144, 6144], P('dp', None, None, 'mp'), may hold values from -6 to 6
- master: float32 [1, 6144, 6144], P(None, 'dp', 'mp'), may hold values from -6 to 6
- momentum: float32 [1, 6144, 6144], P(None, 'dp', 'mp'), may hold values from -4 to 4
Outputs:
- new_master: float32 [1, 6144, 6144], P(None, 'dp', 'mp')
- new_momentum: float32 [1, 6144, 6144], P(None, 'dp', 'mp')
- new_weights: bfloat16 [1, 6144, 6144], P(None, None, 'mp')
All inputs are finite; a program needn't handle non-finite values.
Results may differ from a plain program's by a relative error of at most 0.0014.
Values may be sent and summed in bfloat16 or wider, within the bound.
A program may use at most 128 MiB of HBM per device.

v0:
```python
import jax
import jax.numpy as jnp
from jax import lax
from jax.sharding import PartitionSpec as P

beta_one = 0.9
beta_two = 0.99
step_size = 0.1
decay_rate = 0.1
softness = 0.05


def lion_update(gradient, master, momentum):
    interp = beta_one * momentum + (1.0 - beta_one) * gradient
    direction = interp / jnp.sqrt(interp * interp + softness * softness)
    new_master = master - step_size * (direction + decay_rate * master)
    new_momentum = beta_two * momentum + (1.0 - beta_two) * gradient
    return (new_master, new_momentum)


def per_device(grad_parts, master, momentum):
    replicas = lax.axis_size("dp")
    partials = grad_parts[0].astype(jnp.float32)
    summed = lax.psum_scatter(
        partials.astype(jnp.bfloat16), "dp", scatter_dimension=1, tiled=True
    ).astype(jnp.float32)
    gradient = summed / replicas
    new_master, new_momentum = lion_update(gradient, master, momentum)
    new_weights = lax.all_gather(new_master.astype(jnp.bfloat16), "dp", axis=1, tiled=True)
    return (new_master, new_momentum, new_weights)


def solution(mesh):
    return jax.shard_map(
        per_device,
        mesh=mesh,
        in_specs=(P("dp", None, None, "mp"), P(None, "dp", "mp"), P(None, "dp", "mp")),
        out_specs=(P(None, "dp", "mp"), P(None, "dp", "mp"), P(None, None, "mp")),
        check_vma=False,
    )
```

profile of v0, /device:TPU:0, one launch (start us, length us, event | category | flops | bytes accessed | tf_op | source)
XLA Modules:
  0.0 271.5 jit_solution(14277638528274021986)
XLA Ops:
  7.2 0.0 reduce-scatter.2.cloned.1.call-start
  7.2 0.7 reduce-scatter.2.cloned.1.call-update
  7.9 0.0 all-gather.2.cloned.1.call-start
  7.9 132.9 %reduce-scatter.2.cloned.1.call-done = bf16[1,768,1536]{2,1,0:T(8,128)(2,1)} async-done(((bf16[1,6144,1536]{2,1,0:T(8,128)(2,1)}), bf16[1,768,1536]{2,1,0:T(8,128)(2,1)}) %reduce-scatter.2.cloned.1.call-update) | async-done | bytes 2359312 | tf_op jit(solution)/shard_map/reduce_scatter | solution.py:24
  140.8 8.7 %fusion.2 = (bf16[1,768,1536]{2,1,0:T(8,128)(2,1)}, f32[1,768,1536]{2,1,0:T(8,128)}, f32[1,768,1536]{2,1,0:T(8,128)}) fusion(f32[1,768,1536]{2,1,0:T(8,128)} %param.4, bf16[1,768,1536]{2,1,0:T(8,128)(2,1)} %reduce-scatter.2.cloned.1.call-done, f32[1,768,1536]{2,1,0:T(8,128)} %param.5), kind=kLoop, calls=%fused_computation.5 | loop fusion | flops 17694720 | bytes 23592960 | tf_op jit(solution)/shard_map/convert_element_type | solution.py:29
  149.5 0.0 all-gather.2.cloned.1.call-update
  149.5 98.7 %all-gather.2.cloned.1.call-done = bf16[1,6144,1536]{2,1,0:T(8,128)(2,1)} async-done(((bf16[1,768,1536]{2,1,0:T(8,128)(2,1)}), bf16[1,6144,1536]{2,1,0:T(8,128)(2,1)}) %all-gather.2.cloned.1.call-update) | async-done | bytes 18874384 | tf_op jit(solution)/shard_map/all_gather | solution.py:29
  248.2 16.5 %copy.7 = bf16[1,6144,1536]{2,1,0:T(8,128)(2,1)} copy(bf16[1,6144,1536]{2,1,0:T(8,128)(2,1)} %all-gather.2.cloned.1.call-done) | data formatting | bytes 37748736
Async XLA Ops:
  7.2 133.6 %reduce-scatter.2.cloned.1.call-start = ((), (), s32[]{:S(2)}) async-start(), calls=%async_computation.1 | async-start | bytes 21233664 | tf_op jit(solution)/shard_map/reduce_scatter | solution.py:24
  7.9 240.3 %all-gather.2.cloned.1.call-start = ((), (), s32[]{:S(2)}) async-start(), calls=%async_computation.2 | async-start | bytes 21233664 | tf_op jit(solution)/shard_map/all_gather | solution.py:29
Sparse Core Ops, SparseCore 0:
  11.6 129.1 reduce-scatter.1
  149.6 98.5 all-gather.1
where the time goes:
time: 272 us
  waiting for transfers between devices  232 us (85%)
  local copies, waits for them, and re-layouts  16.5 us (6%)
  between operations  14 us (5%)
  other arithmetic  8.67 us (3%)
    reduce_scatter x1, waiting for transfers between devices, per_device(): lax.psum_scatter(partials.astype(jnp.bfloat16), 'dp', scatter_dimension=1...  133 us
    all_gather x1, waiting for transfers between devices, per_device(): lax.all_gather(new_master.astype(jnp.bfloat16), 'dp', axis=1, tiled=True)  98.7 us
    unnamed x1, local copies, waits for them, and re-layouts  16.5 us
    convert_element_type x1, other arithmetic, per_device(): new_master.astype(jnp.bfloat16)  8.67 us
  transfers between devices with their start and end apart: 2, of which 2 were waited for; matrix products, arithmetic and copies ran while one was open for 0% of the time, Pallas kernels for 0%

commit v1 on v0

v1 whole, which is shorter than its diff:
```python
import functools

import jax
import jax.numpy as jnp
from jax import lax
from jax.experimental import pallas as pl
from jax.experimental.pallas import tpu as pltpu
from jax.sharding import PartitionSpec as P

beta_one = 0.9
beta_two = 0.99
step_size = 0.1
decay_rate = 0.1
softness = 0.05

f32 = jnp.float32
bf16 = jnp.bfloat16
MESH = pl.DeviceIdType.MESH
ROWS = 16
MOST_CHUNKS = 8


def factors(n):
    cores = 2
    across = 2
    return n // (cores * across), across, cores


def kernel(
    dims,
    g_ref, master_ref, momentum_ref,
    nmaster, nmomentum, w,
    own, pair, p1, q1, p2, q2,
    load_sem, state_sem,
    pair_s, pair_r, p1_s, p1_r, q1_s, q1_r, p2_s, p2_r, q2_s, q2_r,
    ay_s, ay_r, ax_s, ax_r, rx_s, rx_r, ry_s, ry_r,
    d0_s, d0_r, dy_s, dy_r, dx_s, dx_r, dp_s, dp_r, dq_s, dq_r,
):
    Y, X, C, K, c = dims
    me = lax.axis_index("dp")
    core = lax.rem(me, C)
    mx = lax.rem(me // C, X)
    my = me // (C * X)
    other = 1 - core

    def index(y, x, k):
        return {"dp": (y * X + x) * C + k}

    mate = index(my, mx, other)

    def plus(a, j, size):
        return lax.rem(a + j, size)

    def minus(a, j, size):
        return lax.rem(a + size - j, size)

    ys, xs = range(1, Y), range(1, X)

    def remote(src, dst, s, r, to):
        return pltpu.make_async_remote_copy(
            src_ref=src, dst_ref=dst, send_sem=s, recv_sem=r,
            device_id=to, device_id_type=MESH,
        )

    def load(k):
        return pltpu.make_async_copy(g_ref.at[:, :, core, :, k], own.at[k], load_sem.at[k])

    def state(k):
        return (
            pltpu.make_async_copy(master_ref.at[:, k], nmaster.at[:, k], state_sem.at[0, k]),
            pltpu.make_async_copy(momentum_ref.at[:, k], nmomentum.at[:, k], state_sem.at[1, k]),
        )

    def pair_copy(k):
        return remote(g_ref.at[:, :, other, :, k], pair.at[k], pair_s.at[k], pair_r.at[k], mate)

    def p1_copy(j, k):
        to = plus(mx, j, X)
        return remote(own.at[k, :, to, 0], p1.at[j - 1, k], p1_s.at[j - 1, k], p1_r.at[j - 1, k], index(my, to, core))

    def q1_copy(j, k):
        to = plus(my, j, Y)
        return remote(own.at[k, to, :, 1], q1.at[j - 1, k], q1_s.at[j - 1, k], q1_r.at[j - 1, k], index(to, mx, core))

    def p2_copy(j, k):
        to = plus(my, j, Y)
        return remote(own.at[k, to, mx, 0], p2.at[j - 1, k], p2_s.at[j - 1, k], p2_r.at[j - 1, k], index(to, mx, core))

    def q2_copy(j, k):
        to = plus(mx, j, X)
        return remote(own.at[k, my, to, 1], q2.at[j - 1, k], q2_s.at[j - 1, k], q2_r.at[j - 1, k], index(my, to, core))

    def spread(block, s, r, to):
        return remote(block, block, s, r, to)

    def ay_copy(j, k, y):
        return spread(w.at[y, mx, core, :, k], ay_s.at[j - 1, k], ay_r.at[j - 1, k], index(plus(my, j, Y), mx, core))

    def ax_copy(j, k, x):
        return spread(w.at[my, x, core, :, k], ax_s.at[j - 1, k], ax_r.at[j - 1, k], index(my, plus(mx, j, X), core))

    def rx_copy(jx, jy, k, x):
        y = minus(my, jy, Y)
        return spread(w.at[y, x, core, 0, k], rx_s.at[jx - 1, jy - 1, k], rx_r.at[jx - 1, jy - 1, k], index(my, plus(mx, jx, X), core))

    def ry_copy(jx, jy, k, y):
        x = minus(mx, jx, X)
        return spread(w.at[y, x, core, 1, k], ry_s.at[jx - 1, jy - 1, k], ry_r.at[jx - 1, jy - 1, k], index(plus(my, jy, Y), mx, core))

    def d0_copy(k, half):
        return spread(w.at[my, mx, half, :, k], d0_s.at[k], d0_r.at[k], mate)

    def dy_copy(j, k, half):
        return spread(w.at[minus(my, j, Y), mx, half, :, k], dy_s.at[j - 1, k], dy_r.at[j - 1, k], mate)

    def dx_copy(j, k, half):
        return spread(w.at[my, minus(mx, j, X), half, :, k], dx_s.at[j - 1, k], dx_r.at[j - 1, k], mate)

    def dp_copy(jx, jy, k, half):
        return spread(w.at[minus(my, jy, Y), minus(mx, jx, X), half, 0, k], dp_s.at[jx - 1, jy - 1, k], dp_r.at[jx - 1, jy - 1, k], mate)

    def dq_copy(jx, jy, k, half):
        return spread(w.at[minus(my, jy, Y), minus(mx, jx, X), half, 1, k], dq_s.at[jx - 1, jy - 1, k], dq_r.at[jx - 1, jy - 1, k], mate)

    def each(body):
        lax.fori_loop(0, K, lambda k, carry: (body(k), carry)[1], 0)

    def rows(body):
        lax.fori_loop(0, c // ROWS, lambda r, carry: (body(pl.ds(pl.multiple_of(r * ROWS, ROWS), ROWS)), carry)[1], 0)

    def start_loads(k):
        load(k).start()

    def start_state(k):
        for copy in state(k):
            copy.start()

    each(start_loads)

    barrier = pltpu.get_barrier_semaphore()
    peers = [mate]
    peers += [index(my, plus(mx, j, X), core) for j in xs]
    peers += [index(plus(my, j, Y), mx, core) for j in ys]
    for peer in peers:
        pl.semaphore_signal(barrier, inc=1, device_id=peer, device_id_type=MESH)
    pl.semaphore_wait(barrier, len(peers))

    each(lambda k: pair_copy(k).start())
    each(start_state)

    def first(k):
        load(k).wait()
        pair_copy(k).wait_recv()

        def add(r):
            for j in xs:
                x = plus(mx, j, X)
                for y in range(Y):
                    own[k, y, x, 0, r] = (own[k, y, x, 0, r].astype(f32) + pair[k, y, x, 0, r].astype(f32)).astype(bf16)
            for j in ys:
                y = plus(my, j, Y)
                for x in range(X):
                    own[k, y, x, 1, r] = (own[k, y, x, 1, r].astype(f32) + pair[k, y, x, 1, r].astype(f32)).astype(bf16)

        rows(add)
        for j in xs:
            p1_copy(j, k).start()
        for j in ys:
            q1_copy(j, k).start()

    each(first)

    def p_sum(k, y, r):
        total = own[k, y, mx, 0, r].astype(f32) + pair[k, y, mx, 0, r].astype(f32)
        for j in xs:
            total += p1[j - 1, k, y, r].astype(f32)
        return total

    def q_sum(k, x, r):
        total = own[k, my, x, 1, r].astype(f32) + pair[k, my, x, 1, r].astype(f32)
        for j in ys:
            total += q1[j - 1, k, x, r].astype(f32)
        return total

    def second(k):
        for j in xs:
            p1_copy(j, k).wait_recv()
        for j in ys:
            q1_copy(j, k).wait_recv()

        def add(r):
            for j in ys:
                y = plus(my, j, Y)
                own[k, y, mx, 0, r] = p_sum(k, y, r).astype(bf16)
            for j in xs:
                x = plus(mx, j, X)
                own[k, my, x, 1, r] = q_sum(k, x, r).astype(bf16)

        rows(add)
        for j in ys:
            p2_copy(j, k).start()
        for j in xs:
            q2_copy(j, k).start()

    each(second)

    def step(total, h, k, r):
        gradient = total * (1.0 / (Y * X * C))
        momentum = nmomentum[h, k, r]
        master = nmaster[h, k, r]
        interp = beta_one * momentum + (1.0 - beta_one) * gradient
        direction = interp * lax.rsqrt(interp * interp + softness * softness)
        new_master = master - step_size * (direction + decay_rate * master)
        nmaster[h, k, r] = new_master
        nmomentum[h, k, r] = beta_two * momentum + (1.0 - beta_two) * gradient
        w[my, mx, core, h, k, r] = new_master.astype(bf16)

    def third(k):
        for copy in state(k):
            copy.wait()
        for j in ys:
            p2_copy(j, k).wait_recv()
        for j in xs:
            q2_copy(j, k).wait_recv()

        def update(r):
            total = p_sum(k, my, r)
            for j in ys:
                total += p2[j - 1, k, r].astype(f32)
            step(total, 0, k, r)
            total = q_sum(k, mx, r)
            for j in xs:
                total += q2[j - 1, k, r].astype(f32)
            step(total, 1, k, r)

        rows(update)
        for j in ys:
            ay_copy(j, k, my).start()
        for j in xs:
            ax_copy(j, k, mx).start()
        d0_copy(k, core).start()

    each(third)

    def fourth(k):
        for jy in ys:
            ay_copy(jy, k, minus(my, jy, Y)).wait_recv()
            for jx in xs:
                rx_copy(jx, jy, k, mx).start()
            dy_copy(jy, k, core).start()
        for jx in xs:
            ax_copy(jx, k, minus(mx, jx, X)).wait_recv()
            for jy in ys:
                ry_copy(jx, jy, k, my).start()
            dx_copy(jx, k, core).start()

    each(fourth)

    def fifth(k):
        for jx in xs:
            for jy in ys:
                rx_copy(jx, jy, k, minus(mx, jx, X)).wait_recv()
                dp_copy(jx, jy, k, core).start()
                ry_copy(jx, jy, k, minus(my, jy, Y)).wait_recv()
                dq_copy(jx, jy, k, core).start()

    each(fifth)

    def finish(k):
        pair_copy(k).wait_send()
        d0_copy(k, other).wait()
        for jx in xs:
            p1_copy(jx, k).wait_send()
            q2_copy(jx, k).wait_send()
            ax_copy(jx, k, mx).wait_send()
            dx_copy(jx, k, other).wait()
            for jy in ys:
                rx_copy(jx, jy, k, mx).wait_send()
                ry_copy(jx, jy, k, my).wait_send()
                dp_copy(jx, jy, k, other).wait()
                dq_copy(jx, jy, k, other).wait()
        for jy in ys:
            q1_copy(jy, k).wait_send()
            p2_copy(jy, k).wait_send()
            ay_copy(jy, k, my).wait_send()
            dy_copy(jy, k, other).wait()

    each(finish)


def per_device(n, grad_parts, master, momentum):
    Y, X, C = factors(n)
    layers, rows, cols = master.shape
    tall = layers * rows
    half = tall // 2
    K = max(k for k in range(1, MOST_CHUNKS + 1) if half % (k * ROWS) == 0)
    c = half // K
    g = grad_parts.reshape(Y, X, C, 2, K, c, cols)
    state_shape = (2, K, c, cols)
    w_shape = (Y, X, C, 2, K, c, cols)
    scratch = [
        (K, Y, X, 2, c, cols), (K, Y, X, 2, c, cols),
        (X - 1, K, Y, c, cols), (Y - 1, K, X, c, cols),
        (Y - 1, K, c, cols), (X - 1, K, c, cols),
    ]
    sems = [(K,), (2, K)]
    for shape in ((K,), (X - 1, K), (Y - 1, K), (Y - 1, K), (X - 1, K),
                  (Y - 1, K), (X - 1, K), (X - 1, Y - 1, K), (X - 1, Y - 1, K),
                  (K,), (Y - 1, K), (X - 1, K), (X - 1, Y - 1, K), (X - 1, Y - 1, K)):
        sems += [shape, shape]
    size = lambda s: functools.reduce(lambda a, b: a * b, s)
    new_master, new_momentum, weights = pl.pallas_call(
        functools.partial(kernel, (Y, X, C, K, c)),
        out_shape=(
            pltpu.VMEM(state_shape, f32),
            pltpu.VMEM(state_shape, f32),
            pltpu.VMEM(w_shape, bf16),
        ),
        in_specs=[pl.BlockSpec(memory_space=pltpu.HBM)] * 3,
        out_specs=[pl.BlockSpec(memory_space=pltpu.VMEM)] * 3,
        scratch_shapes=[pltpu.VMEM(s, bf16) for s in scratch]
        + [pltpu.SemaphoreType.DMA(s) for s in sems],
        compiler_params=pltpu.CompilerParams(
            collective_id=0, has_side_effects=True,
            vmem_limit_bytes=sum(2 * size(s) for s in scratch) + (2 << 20),
        ),
    )(g, master.reshape(state_shape), momentum.reshape(state_shape))
    return (
        new_master.reshape(master.shape),
        new_momentum.reshape(master.shape),
        weights.reshape(layers, n * rows, cols),
    )


def solution(mesh):
    return jax.shard_map(
        functools.partial(per_device, mesh.shape["dp"]),
        mesh=mesh,
        in_specs=(P("dp", None, None, "mp"), P(None, "dp", "mp"), P(None, "dp", "mp")),
        out_specs=(P(None, "dp", "mp"), P(None, "dp", "mp"), P(None, None, "mp")),
        check_vma=False,
    )
```

time: 272 us -> 175 us (0.64)
  waiting for transfers between devices: 232 us -> 0 us
  Pallas kernels: 0 us -> 163 us
  between operations: 14 us -> 0.64 us
  other arithmetic: 8.67 us -> 0 us
  local copies, waits for them, and re-layouts: 16.5 us -> 11.2 us
    pallas_call x0 -> x1, Pallas kernels: none -> 163 us  [per_device(): pl.pallas_call(functools.partial(kernel, (Y, X, C, K, c)), out_shape=(plt...]
    reduce_scatter x1 -> x0, waiting for transfers between devices: 133 us -> none  [per_device(): lax.psum_scatter(partials.astype(jnp.bfloat16), 'dp', scatter_dimension=1...]
    all_gather x1 -> x0, waiting for transfers between devices: 98.7 us -> none  [per_device(): lax.all_gather(new_master.astype(jnp.bfloat16), 'dp', axis=1, tiled=True)]
    convert_element_type x1 -> x0, other arithmetic: 8.67 us -> none  [per_device(): new_master.astype(jnp.bfloat16)]
    unnamed x1 -> x3, local copies, waits for them, and re-layouts: 16.5 us -> 11.2 us
  transfers between devices with their start and end apart: 2 -> 0, of which waited for: 2 -> 0; matrix products, arithmetic and copies ran while one was open for 0% -> 0% of each run, Pallas kernels for 0% -> 0%
where the time goes in v1:
time: 175 us
  Pallas kernels  163 us (93%)
  local copies, waits for them, and re-layouts  11.2 us (6%)
    pallas_call x1, Pallas kernels, per_device(): pl.pallas_call(functools.partial(kernel, (Y, X, C, K, c)), out_shape=(plt...  163 us
    unnamed x3, local copies, waits for them, and re-layouts  11.2 us

profile of v1, /device:TPU:0, one launch (start us, length us, event | category | flops | bytes accessed | tf_op | source)
XLA Modules:
  0.0 175.2 jit_solution(11156117827063751880)
XLA Ops:
  0.6 163.3 %shard_map.58 = (f32[2,8,48,1536]{3,2,1,0:T(8,128)S(1)}, f32[2,8,48,1536]{3,2,1,0:T(8,128)S(1)}, bf16[2,2,2,2,8,48,1536]{6,5,4,3,2,1,0:T(8,128)(2,1)S(1)}) custom-call(bf16[2,2,2,2,8,48,1536]{6,5,4,3,2,1,0:T(8,128)(2,1)} %bitcast.9, f32[2,8,48,1536]{3,2,1,0:T(8,128)} %bitcast.10, f32[2,8,48,1536]{3,2,1,0:T(8,128)} %bitcast.11), custom_call_target="tpu_custom_call" | custom-call | tf_op jit(solution)/shard_map/pallas_call | solution.py:312
  163.9 2.2 %copy.9 = f32[1,768,1536]{2,1,0:T(8,128)} copy(f32[1,768,1536]{2,1,0:T(8,128)S(1)} %bitcast.8) | data formatting | bytes 9437184
  166.1 2.2 %copy.10 = f32[1,768,1536]{2,1,0:T(8,128)} copy(f32[1,768,1536]{2,1,0:T(8,128)S(1)} %bitcast.7) | data formatting | bytes 9437184
  168.3 6.8 %copy.11 = bf16[1,6144,1536]{2,1,0:T(8,128)(2,1)} copy(bf16[1,6144,1536]{2,1,0:T(8,128)(2,1)S(1)} %bitcast.6) | data formatting | bytes 37748736

commit v2 on v1

--- a/solution.py
+++ b/solution.py
@@ -286,6 +286,34 @@
             dy_copy(jy, k, other).wait()
 
     each(finish)
+
+
+def put_kernel(pieces, *refs):
+    sources, targets, sem = refs[:3], refs[3:6], refs[6]
+    copies = []
+    for source, target, cut in zip(sources, targets, pieces):
+        for at in cut:
+            copies.append(pltpu.make_async_copy(source.at[at], target.at[at], sem.at[len(copies)]))
+    for copy in copies:
+        copy.start()
+    for copy in copies:
+        copy.wait()
+
+
+def put(arrays):
+    depths = (1, 1, 3)
+    pieces = [[()] for _ in arrays]
+    for i, depth in enumerate(depths):
+        for d in range(depth):
+            pieces[i] = [at + (k,) for at in pieces[i] for k in range(arrays[i].shape[d])]
+    return pl.pallas_call(
+        functools.partial(put_kernel, pieces),
+        out_shape=[jax.ShapeDtypeStruct(a.shape, a.dtype) for a in arrays],
+        in_specs=[pl.BlockSpec(memory_space=pltpu.VMEM)] * len(arrays),
+        out_specs=[pl.BlockSpec(memory_space=pltpu.HBM)] * len(arrays),
+        scratch_shapes=[pltpu.SemaphoreType.DMA((sum(len(cut) for cut in pieces),))],
+        compiler_params=pltpu.CompilerParams(vmem_limit_bytes=1 << 20),
+    )(*arrays)
 
 
 def per_device(n, grad_parts, master, momentum):
@@ -309,7 +337,7 @@
                   (K,), (Y - 1, K), (X - 1, K), (X - 1, Y - 1, K), (X - 1, Y - 1, K)):
         sems += [shape, shape]
     size = lambda s: functools.reduce(lambda a, b: a * b, s)
-    new_master, new_momentum, weights = pl.pallas_call(
+    results = pl.pallas_call(
         functools.partial(kernel, (Y, X, C, K, c)),
         out_shape=(
             pltpu.VMEM(state_shape, f32),
@@ -325,6 +353,7 @@
             vmem_limit_bytes=sum(2 * size(s) for s in scratch) + (2 << 20),
         ),
     )(g, master.reshape(state_shape), momentum.reshape(state_shape))
+    new_master, new_momentum, weights = put(results)
     return (
         new_master.reshape(master.shape),
         new_momentum.reshape(master.shape),

time: 175 us -> 174 us (level)
  local copies, waits for them, and re-layouts: 11.2 us -> 0 us
  Pallas kernels: 163 us -> 173 us
    unnamed x3 -> x0, local copies, waits for them, and re-layouts: 11.2 us -> none
    pallas_call x0 -> x1, Pallas kernels: none -> 9.45 us  [put(): pl.pallas_call(functools.partial(put_kernel, pieces), out_shape=[jax.Shap...]
where the time goes in v2:
time: 174 us; the launch traced here: 173 us
  Pallas kernels  173 us (99%)
    pallas_call x1, Pallas kernels, per_device(): pl.pallas_call(functools.partial(kernel, (Y, X, C, K, c)), out_shape=(plt...  163 us
    pallas_call x1, Pallas kernels, put(): pl.pallas_call(functools.partial(put_kernel, pieces), out_shape=[jax.Shap...  9.45 us

profile of v2, /device:TPU:0, one launch (start us, length us, event | category | flops | bytes accessed | tf_op | source)
XLA Modules:
  0.0 173.4 jit_solution(13392387520870771866)
XLA Ops:
  0.6 163.3 %shard_map.58 = (f32[2,8,48,1536]{3,2,1,0:T(8,128)S(1)}, f32[2,8,48,1536]{3,2,1,0:T(8,128)S(1)}, bf16[2,2,2,2,8,48,1536]{6,5,4,3,2,1,0:T(8,128)(2,1)S(1)}) custom-call(bf16[2,2,2,2,8,48,1536]{6,5,4,3,2,1,0:T(8,128)(2,1)} %bitcast.6, f32[2,8,48,1536]{3,2,1,0:T(8,128)} %bitcast.7, f32[2,8,48,1536]{3,2,1,0:T(8,128)} %bitcast.8), custom_call_target="tpu_custom_call" | custom-call | tf_op jit(solution)/shard_map/pallas_call | solution.py:340
  163.9 9.5 %shard_map.59 = (f32[2,8,48,1536]{3,2,1,0:T(8,128)}, f32[2,8,48,1536]{3,2,1,0:T(8,128)}, bf16[2,2,2,2,8,48,1536]{6,5,4,3,2,1,0:T(8,128)(2,1)}) custom-call(f32[2,8,48,1536]{3,2,1,0:T(8,128)S(1)} %get-tuple-element.9.refs_0_, f32[2,8,48,1536]{3,2,1,0:T(8,128)S(1)} %get-tuple-element.10.refs_1_, bf16[2,2,2,2,8,48,1536]{6,5,4,3,2,1,0:T(8,128)(2,1)S(1)} %get-tuple-element.11.refs_2_), custom_call_target="tpu_custom_call" | custom-call | tf_op jit(solution)/shard_map/pallas_call | solution.py:309
